TPU v7x, 32 devices: a whole 2x2x4 slice. The times are simulated.
32 devices in a mesh: tok: 8 (over y, x, core), blk: 4 (over z).
Axes of the slice: x: 2, y: 2, z: 4, core: 2. Of those that a mesh axis runs over, the one named last changes fastest.
Arguments:
- activations: bfloat16 [4096, 4096], P('tok', 'blk'), may hold values from -52 to 52, as said below
- out_grads: bfloat16 [4096, 4096], P('tok', 'blk'), may hold values from -52 to 52, as said below
Outputs:
- act_inverse: float32 [4096, 4096], P(('tok', 'blk'))
- grad_inverse: float32 [4096, 4096], P(('tok', 'blk'))
Inputs may be any that keep to these rules, and one draw needn't show every extreme that they name: `activations`: real entries. `out_grads`: real entries.
All inputs are finite; a program needn't handle non-finite values.
Results may differ from a plain program's by a relative error of at most 0.02.
Values may be sent and summed in bfloat16 or wider, within the bound.
A program may use at most 64 MiB of HBM per device.

v0:
```python
import jax
import jax.numpy as jnp
from jax import lax
from jax.sharding import PartitionSpec as P

D = 4096
damping = 0.3
epsilon = 1e-06
divisor = 2.0


def column_squares(data):
    values = data.astype(jnp.float32)
    return jnp.sum(values * values, axis=0)


def fold_product(row_block, tile):
    return jnp.dot(
        row_block,
        lax.all_gather(tile, "tok", axis=0, tiled=True),
        preferred_element_type=jnp.float32,
    )


def newton_steps(scaled, identity):
    half = scaled.astype(jnp.bfloat16)
    row_block = lax.all_gather(half, "blk", axis=1, tiled=True)
    square = fold_product(row_block, half)
    cube = fold_product(row_block, square.astype(jnp.bfloat16))
    return 4.0 * identity - 6.0 * scaled + 4.0 * square - cube


def body(activations, out_grads):
    tok_count = lax.axis_size("tok")
    blk_count = lax.axis_size("blk")
    tok_id = lax.axis_index("tok")
    blk_id = lax.axis_index("blk")
    token_count = activations.shape[0] * tok_count
    tile_rows = D // tok_count
    tile_cols = D // blk_count
    full_acts, full_grads = (
        lax.all_gather(activations, "blk", axis=1, tiled=True),
        lax.all_gather(out_grads, "blk", axis=1, tiled=True),
    )
    sums_act, sums_grad = (
        lax.psum(column_squares(full_acts).astype(jnp.bfloat16), "tok").astype(jnp.float32),
        lax.psum(column_squares(full_grads).astype(jnp.bfloat16), "tok").astype(jnp.float32),
    )
    row_ids = tok_id * tile_rows + jnp.arange(tile_rows, dtype=jnp.int32)
    col_ids = blk_id * tile_cols + jnp.arange(tile_cols, dtype=jnp.int32)
    identity = (row_ids[:, None] == col_ids[None, :]).astype(jnp.float32)

    def damped_tile(full, local, sums):
        gram_tile = lax.psum_scatter(
            lax.dot_general(
                full, local, (((0,), (0,)), ((), ())), preferred_element_type=jnp.float32
            ).astype(jnp.bfloat16),
            "tok",
            scatter_dimension=0,
            tiled=True,
        ).astype(jnp.float32)
        inverse = lax.rsqrt(sums / token_count + epsilon)
        inverse_rows = lax.dynamic_slice_in_dim(inverse, tok_id * tile_rows, tile_rows)
        inverse_cols = lax.dynamic_slice_in_dim(inverse, blk_id * tile_cols, tile_cols)
        return (
            gram_tile / token_count * inverse_rows[:, None] * inverse_cols[None, :]
            + damping * identity
        )

    damped_act = damped_tile(full_acts, activations, sums_act)
    damped_grad = damped_tile(full_grads, out_grads, sums_grad)
    results = []
    for damped in (damped_act, damped_grad):
        scaled = damped / divisor
        result_tile = newton_steps(scaled, identity)
        results.append(
            lax.all_to_all(
                result_tile.astype(jnp.bfloat16), "blk", split_axis=0, concat_axis=1, tiled=True
            ).astype(result_tile.dtype)
        )
    return (results[0], results[1])


def solution(mesh):
    placed = (P("tok", "blk"), P("tok", "blk"))
    return jax.shard_map(
        body,
        mesh=mesh,
        in_specs=placed,
        out_specs=(P(("tok", "blk"), None), P(("tok", "blk"), None)),
        check_vma=False,
    )
```

profile of v0, /device:TPU:0, one launch (start us, length us, event | category | flops | bytes accessed | tf_op | source)
XLA Modules:
  0.0 763.5 jit_solution(1316433522095304969)
XLA Ops:
  7.2 0.0 all-gather.9.cloned.1.call-start
  7.2 0.7 all-gather.9.cloned.1.call-update
  7.9 0.0 all-gather.17.cloned.1.call-start
  8.0 0.7 all-gather.17.cloned.1.call-update
  8.7 0.0 reduce-scatter.3.cloned.1.call-start
  8.7 84.3 %all-gather.9.cloned.1.call-done = bf16[512,4096]{1,0:T(8,128)(2,1)} async-done(((bf16[512,1024]{1,0:T(8,128)(2,1)}), bf16[512,4096]{1,0:T(8,128)(2,1)}) %all-gather.9.cloned.1.call-update) | async-done | bytes 4194320 | tf_op jit(solution)/shard_map/all_gather | solution.py:42
  93.0 9.1 %convolution_convert_fusion.1 = bf16[4096,1024]{1,0:T(8,128)(2,1)} fusion(bf16[512,4096]{1,0:T(8,128)(2,1)} %all-gather.9.cloned.1.call-done, bf16[512,1024]{1,0:T(8,128)(2,1)S(1)} %copy-done.1), kind=kOutput, calls=%fused_computation.3 | convolution fusion | flops 4299161600 | bytes 13631488 | tf_op jit(solution)/shard_map/dot_general | solution.py:55
  102.1 0.0 reduce-scatter.3.cloned.1.call-update
  102.2 0.0 reduce-scatter.5.cloned.1.call-start
  102.2 71.7 %all-gather.17.cloned.1.call-done = bf16[512,4096]{1,0:T(8,128)(2,1)} async-done(((bf16[512,1024]{1,0:T(8,128)(2,1)}), bf16[512,4096]{1,0:T(8,128)(2,1)}) %all-gather.17.cloned.1.call-update) | async-done | bytes 4194320 | tf_op jit(solution)/shard_map/all_gather | solution.py:43
  173.9 9.0 %convolution_convert_fusion = bf16[4096,1024]{1,0:T(8,128)(2,1)} fusion(bf16[512,4096]{1,0:T(8,128)(2,1)} %all-gather.17.cloned.1.call-done, bf16[512,1024]{1,0:T(8,128)(2,1)S(1)} %copy-done.2), kind=kOutput, calls=%fused_computation.2 | convolution fusion | flops 4299161600 | bytes 13631488 | tf_op jit(solution)/shard_map/dot_general | solution.py:55
  182.9 0.0 reduce-scatter.5.cloned.1.call-update
  182.9 0.0 all-gather.19.cloned.1.call-start
  183.0 4.2 multiply_reduce_fusion
  187.1 1.0 copy-done
  188.2 0.9 multiply_reduce_fusion.1
  189.1 24.5 %all-reduce = (bf16[4096]{0:T(1024)(128)(2,1)S(1)}, bf16[4096]{0:T(1024)(128)(2,1)S(1)}) all-reduce(bf16[4096]{0:T(1024)(128)(2,1)S(1)} %multiply_reduce_fusion.1, bf16[4096]{0:T(1024)(128)(2,1)S(1)} %multiply_reduce_fusion), channel_id=1, replica_groups=mesh['tok'=8,'blk'=4] {'tok'}, use_global_device_ids=true, to_apply=%region_2.0 | all-reduce | flops 8192 | bytes 32768 | tf_op jit(solution)/shard_map/psum | solution.py:46
  213.6 0.1 dynamic-slice_multiply_fusion
  213.7 0.1 dynamic-slice_multiply_fusion.1
  213.8 33.8 %reduce-scatter.3.cloned.1.call-done = bf16[512,1024]{1,0:T(8,128)(2,1)} async-done(((bf16[4096,1024]{1,0:T(8,128)(2,1)}), bf16[512,1024]{1,0:T(8,128)(2,1)}) %reduce-scatter.3.cloned.1.call-update) | async-done | bytes 1048592 | tf_op jit(solution)/shard_map/reduce_scatter | solution.py:54
  247.6 74.8 %reduce-scatter.5.cloned.1.call-done = bf16[512,1024]{1,0:T(8,128)(2,1)} async-done(((bf16[4096,1024]{1,0:T(8,128)(2,1)}), bf16[512,1024]{1,0:T(8,128)(2,1)}) %reduce-scatter.5.cloned.1.call-update) | async-done | bytes 1048592 | tf_op jit(solution)/shard_map/reduce_scatter | solution.py:54
  322.4 3.8 multiply_convert_fusion
  326.2 0.0 all-gather.21.cloned.1.call-start
  326.3 0.5 all-gather.21.cloned.1.call-update
  326.8 0.0 all-gather.11.cloned.1.call-start
  326.9 0.7 all-gather.11.cloned.1.call-update
  327.6 0.0 all-gather.13.cloned.1.call-start
  327.6 0.7 all-gather.13.cloned.1.call-update
  328.3 0.0 all-gather.23.cloned.1.call-start
  328.4 78.8 %all-gather.19.cloned.1.call-done = bf16[512,4096]{1,0:T(8,128)(2,1)} async-done(((bf16[512,1024]{1,0:T(8,128)(2,1)}), bf16[512,4096]{1,0:T(8,128)(2,1)}) %all-gather.19.cloned.1.call-update) | async-done | bytes 4194320 | tf_op jit(solution)/shard_map/all_gather | solution.py:27
  407.1 55.1 %all-gather.21.cloned.1.call-done = bf16[4096,1024]{1,0:T(8,128)(2,1)} async-done(((bf16[512,1024]{1,0:T(8,128)(2,1)}), bf16[4096,1024]{1,0:T(8,128)(2,1)}) %all-gather.21.cloned.1.call-update) | async-done | bytes 8388624 | tf_op jit(solution)/shard_map/all_gather | solution.py:20
  462.2 10.1 %fusion.9 = (bf16[512,1024]{1,0:T(8,128)(2,1)}, f32[512,1024]{1,0:T(8,128)S(1)}) fusion(bf16[512,4096]{1,0:T(8,128)(2,1)} %all-gather.19.cloned.1.call-done, bf16[4096,1024]{1,0:T(8,128)(2,1)} %all-gather.21.cloned.1.call-done), kind=kOutput, calls=%fused_computation.26 | convolution fusion | flops 4295491584 | bytes 15728640 | tf_op jit(solution)/shard_map/dot_general | solution.py:18
  472.4 0.0 all-gather.23.cloned.1.call-update
  472.4 0.2 all-gather.15.cloned.1.call-start
  472.6 72.5 %all-gather.11.cloned.1.call-done = bf16[512,4096]{1,0:T(8,128)(2,1)} async-done(((bf16[512,1024]{1,0:T(8,128)(2,1)}), bf16[512,4096]{1,0:T(8,128)(2,1)}) %all-gather.11.cloned.1.call-update) | async-done | bytes 4194320 | tf_op jit(solution)/shard_map/all_gather | solution.py:27
  545.1 55.2 %all-gather.13.cloned.1.call-done = bf16[4096,1024]{1,0:T(8,128)(2,1)} async-done(((bf16[512,1024]{1,0:T(8,128)(2,1)}), bf16[4096,1024]{1,0:T(8,128)(2,1)}) %all-gather.13.cloned.1.call-update) | async-done | bytes 8388624 | tf_op jit(solution)/shard_map/all_gather | solution.py:20
  600.4 10.8 %fusion.8 = (bf16[512,1024]{1,0:T(8,128)(2,1)}, f32[512,1024]{1,0:T(8,128)}) fusion(bf16[512,4096]{1,0:T(8,128)(2,1)} %all-gather.11.cloned.1.call-done, bf16[4096,1024]{1,0:T(8,128)(2,1)} %all-gather.13.cloned.1.call-done), kind=kOutput, calls=%fused_computation.25 | convolution fusion | flops 4295491584 | bytes 15728640 | tf_op jit(solution)/shard_map/dot_general | solution.py:18
  611.2 45.4 %all-gather.23.cloned.1.call-done = bf16[4096,1024]{1,0:T(8,128)(2,1)} async-done(((bf16[512,1024]{1,0:T(8,128)(2,1)}), bf16[4096,1024]{1,0:T(8,128)(2,1)}) %all-gather.23.cloned.1.call-update) | async-done | bytes 8388624 | tf_op jit(solution)/shard_map/all_gather | solution.py:20
  656.6 10.6 %fusion.7 = bf16[512,1024]{1,0:T(8,128)(2,1)} fusion(f32[512,1024]{1,0:T(8,128)S(1)} %get-tuple-element.9, bf16[512,1024]{1,0:T(8,128)(2,1)S(1)} %copy-done.4, bf16[512,4096]{1,0:T(8,128)(2,1)} %all-gather.19.cloned.1.call-done, bf16[4096,1024]{1,0:T(8,128)(2,1)} %all-gather.23.cloned.1.call-done, f32[1024]{0:T(1024)S(1)} %dynamic_slice.15, ...), kind=kOutput, calls=%fused_computation.14 | convolution fusion | flops 4301783040 | bytes 16789504 | tf_op jit(solution)/shard_map/dot_general | solution.py:18
  667.2 4.7 all-to-all-start.1
  671.9 41.2 %all-gather.15.cloned.1.call-done = bf16[4096,1024]{1,0:T(8,128)(2,1)} async-done(((bf16[512,1024]{1,0:T(8,128)(2,1)}), bf16[4096,1024]{1,0:T(8,128)(2,1)}) %all-gather.15.cloned.1.call-update) | async-done | bytes 8388624 | tf_op jit(solution)/shard_map/all_gather | solution.py:20
  713.2 11.1 %fusion.4 = bf16[512,1024]{1,0:T(8,128)(2,1)} fusion(f32[512,1024]{1,0:T(8,128)} %get-tuple-element.7, bf16[512,1024]{1,0:T(8,128)(2,1)S(1)} %copy-done.3, bf16[512,4096]{1,0:T(8,128)(2,1)} %all-gather.11.cloned.1.call-done, bf16[4096,1024]{1,0:T(8,128)(2,1)} %all-gather.15.cloned.1.call-done, f32[1024]{0:T(1024)S(1)} %dynamic_slice.13, ...), kind=kOutput, calls=%fused_computation.11 | convolution fusion | flops 4301783040 | bytes 16789504 | tf_op jit(solution)/shard_map/dot_general | solution.py:18
  724.3 4.6 all-to-all-start
  728.9 0.2 convert_bitcast_fusion
  729.1 1.5 copy.7
  730.6 24.4 %all-to-all-done = bf16[4,128,1024]{2,1,0:T(8,128)(2,1)S(1)} async-done(((bf16[4,128,1024]{2,1,0:T(8,128)(2,1)}), bf16[4,128,1024]{2,1,0:T(8,128)(2,1)S(1)}, u32[]{:S(2)}, u32[]{:S(2)}) %all-to-all-start) | async-done | bytes 1048608 | tf_op jit(solution)/shard_map/all_to_all | solution.py:77
  755.0 0.2 convert_bitcast_fusion.1
  755.2 1.5 copy.6
  (17 shorter events, 0.1 us)
Async XLA Ops:
  7.2 85.9 %copy-start.1 = (bf16[512,1024]{1,0:T(8,128)(2,1)S(1)}, bf16[512,1024]{1,0:T(8,128)(2,1)}, u32[]{:S(2)}) copy-start(bf16[512,1024]{1,0:T(8,128)(2,1)} %param.2) | copy-start | bytes 3145732
  7.2 85.9 %all-gather.9.cloned.1.call-start = ((), (), s32[]{:S(2)}) async-start(), calls=%async_computation.4 | async-start | bytes 5242880 | tf_op jit(solution)/shard_map/all_gather | solution.py:42
  7.9 166.0 %all-gather.17.cloned.1.call-start = ((), (), s32[]{:S(2)}) async-start(), calls=%async_computation.9 | async-start | bytes 5242880 | tf_op jit(solution)/shard_map/all_gather | solution.py:43
  8.7 238.9 %reduce-scatter.3.cloned.1.call-start = ((), (), s32[]{:S(2)}) async-start(), calls=%async_computation.5 | async-start | bytes 9437184 | tf_op jit(solution)/shard_map/reduce_scatter | solution.py:54
  102.1 71.7 %copy-start.2 = (bf16[512,1024]{1,0:T(8,128)(2,1)S(1)}, bf16[512,1024]{1,0:T(8,128)(2,1)}, u32[]{:S(2)}) copy-start(bf16[512,1024]{1,0:T(8,128)(2,1)} %param.3) | copy-start | bytes 3145732
  102.2 220.2 %reduce-scatter.5.cloned.1.call-start = ((), (), s32[]{:S(2)}) async-start(), calls=%async_computation.10 | async-start | bytes 9437184 | tf_op jit(solution)/shard_map/reduce_scatter | solution.py:54
  182.9 224.3 %all-gather.19.cloned.1.call-start = ((), (), s32[]{:S(2)}) async-start(), calls=%async_computation.11 | async-start | bytes 5242880 | tf_op jit(solution)/shard_map/all_gather | solution.py:27
  183.0 5.2 copy-start
  326.2 136.0 %all-gather.21.cloned.1.call-start = ((), (), s32[]{:S(2)}) async-start(), calls=%async_computation.12 | async-start | bytes 9437184 | tf_op jit(solution)/shard_map/all_gather | solution.py:20
  326.8 218.3 %all-gather.11.cloned.1.call-start = ((), (), s32[]{:S(2)}) async-start(), calls=%async_computation.6 | async-start | bytes 5242880 | tf_op jit(solution)/shard_map/all_gather | solution.py:27
  327.6 272.8 %all-gather.13.cloned.1.call-start = ((), (), s32[]{:S(2)}) async-start(), calls=%async_computation.7 | async-start | bytes 9437184 | tf_op jit(solution)/shard_map/all_gather | solution.py:20
  328.3 328.3 %all-gather.23.cloned.1.call-start = ((), (), s32[]{:S(2)}) async-start(), calls=%async_computation.13 | async-start | bytes 9437184 | tf_op jit(solution)/shard_map/all_gather | solution.py:20
  472.4 184.2 %copy-start.4 = (bf16[512,1024]{1,0:T(8,128)(2,1)S(1)}, bf16[512,1024]{1,0:T(8,128)(2,1)}, u32[]{:S(2)}) copy-start(bf16[512,1024]{1,0:T(8,128)(2,1)} %reduce-scatter.5.cloned.1.call-done) | copy-start | bytes 3145732
  472.4 240.8 %all-gather.15.cloned.1.call-start = ((), (), s32[]{:S(2)}) async-start(), calls=%async_computation.8 | async-start | bytes 9437184 | tf_op jit(solution)/shard_map/all_gather | solution.py:20
  667.2 46.0 %copy-start.3 = (bf16[512,1024]{1,0:T(8,128)(2,1)S(1)}, bf16[512,1024]{1,0:T(8,128)(2,1)}, u32[]{:S(2)}) copy-start(bf16[512,1024]{1,0:T(8,128)(2,1)} %reduce-scatter.3.cloned.1.call-done) | copy-start | bytes 3145732
  667.2 57.0 %all-to-all-start.1 = ((bf16[4,128,1024]{2,1,0:T(8,128)(2,1)}), bf16[4,128,1024]{2,1,0:T(8,128)(2,1)S(1)}, u32[]{:S(2)}, u32[]{:S(2)}) async-start(bf16[4,128,1024]{2,1,0:T(8,128)(2,1)} %bitcast.2), calls=%async_computation.3 | async-start | bytes 2097152 | tf_op jit(solution)/shard_map/all_to_all | solution.py:77
  724.3 30.7 %all-to-all-start = ((bf16[4,128,1024]{2,1,0:T(8,128)(2,1)}), bf16[4,128,1024]{2,1,0:T(8,128)(2,1)S(1)}, u32[]{:S(2)}, u32[]{:S(2)}) async-start(bf16[4,128,1024]{2,1,0:T(8,128)(2,1)} %bitcast), calls=%async_computation.1 | async-start | bytes 2097152 | tf_op jit(solution)/shard_map/all_to_all | solution.py:77
Sparse Core Ops, SparseCore 0:
  9.6 83.4 all-gather.8
  94.6 79.2 all-gather.16
  177.3 70.1 reduce-scatter.2
  250.9 71.4 reduce-scatter.4
  326.4 80.7 all-gather.18
  409.5 52.7 all-gather.20
  464.4 80.7 all-gather.10
  547.6 52.7 all-gather.12
  602.3 54.2 all-gather.22
  658.9 54.2 all-gather.14
where the time goes:
time: 764 us
  waiting for transfers between devices  641 us (84%)
  matrix products  60.7 us (8%)
  blocking collectives  24.5 us (3%)
  between operations  14.3 us (2%)
  starting transfers between devices  9.9 us (1%)
  other arithmetic  9.53 us (1%)
    all_gather x4, waiting for transfers between devices, fold_product(): lax.all_gather(tile, 'tok', axis=0, tiled=True)  197 us
    all_gather x2, waiting for transfers between devices, newton_steps(): row_block = lax.all_gather(half, 'blk', axis=1, tiled=True)  151 us
    reduce_scatter x2, waiting for transfers between devices, damped_tile(): lax.psum_scatter(lax.dot_general(full, local, (((0,), (0,)), ((), ())), p...  109 us
    all_gather x1, waiting for transfers between devices, body(): lax.all_gather(activations, 'blk', axis=1, tiled=True)  84.3 us
    all_gather x1, waiting for transfers between devices, body(): lax.all_gather(out_grads, 'blk', axis=1, tiled=True)  71.7 us
    dot_general x4, matrix products, fold_product(): jnp.dot(row_block, lax.all_gather(tile, 'tok', axis=0, tiled=True), prefe...  42.6 us
    psum x1, blocking collectives, body(): lax.psum(column_squares(full_acts).astype(jnp.bfloat16), 'tok')  24.5 us
    all_to_all x2, waiting for transfers between devices, body(): lax.all_to_all(result_tile.astype(jnp.bfloat16), 'blk', split_axis=0, con...  24.4 us
  transfers between devices with their start and end apart: 12, of which 11 were waited for; matrix products, arithmetic and copies ran while one was open for 9% of the time, Pallas kernels for 0%

commit v1 on v0

--- a/solution.py
+++ b/solution.py
@@ -24,7 +24,7 @@
 
 def newton_steps(scaled, identity):
     half = scaled.astype(jnp.bfloat16)
-    row_block = lax.all_gather(half, "blk", axis=1, tiled=True)
+    row_block = jnp.concatenate(lax.all_gather(half, "blk"), axis=1)
     square = fold_product(row_block, half)
     cube = fold_product(row_block, square.astype(jnp.bfloat16))
     return 4.0 * identity - 6.0 * scaled + 4.0 * square - cube

time: 764 us -> 763 us (level)
  waiting for transfers between devices: 641 us -> 625 us
  local copies, waits for them, and re-layouts: 4 us -> 16.4 us
    all_gather x4, waiting for transfers between devices: 197 us -> 183 us  [fold_product(): lax.all_gather(tile, 'tok', axis=0, tiled=True)]
    all_gather x0 -> x2, local copies, waits for them, and re-layouts: none -> 12.4 us  [newton_steps(): row_block = jnp.concatenate(lax.all_gather(half, 'blk'), axis=1)]
  transfers between devices with their start and end apart: 12 -> 12, of which waited for: 11 -> 11; matrix products, arithmetic and copies ran while one was open for 9% -> 11% of each run, Pallas kernels for 0% -> 0%
where the time goes in v1:
time: 763 us; the launch traced here: 762 us
  waiting for transfers between devices  625 us (82%)
  matrix products  62.2 us (8%)
  blocking collectives  24.5 us (3%)
  local copies, waits for them, and re-layouts  16.4 us (2%)
  between operations  14.3 us (2%)
  starting transfers between devices  9.91 us (1%)
  other arithmetic  9.57 us (1%)
    all_gather x4, waiting for transfers between devices, fold_product(): lax.all_gather(tile, 'tok', axis=0, tiled=True)  183 us
    all_gather x2, waiting for transfers between devices, newton_steps(): row_block = jnp.concatenate(lax.all_gather(half, 'blk'), axis=1)  150 us
    reduce_scatter x2, waiting for transfers between devices, damped_tile(): lax.psum_scatter(lax.dot_general(full, local, (((0,), (0,)), ((), ())), p...  109 us
    all_gather x1, waiting for transfers between devices, body(): lax.all_gather(activations, 'blk', axis=1, tiled=True)  84.3 us
    all_gather x1, waiting for transfers between devices, body(): lax.all_gather(out_grads, 'blk', axis=1, tiled=True)  71.6 us
    dot_general x4, matrix products, fold_product(): jnp.dot(row_block, lax.all_gather(tile, 'tok', axis=0, tiled=True), prefe...  44.1 us
    psum x1, blocking collectives, body(): lax.psum(column_squares(full_acts).astype(jnp.bfloat16), 'tok')  24.5 us
    all_to_all x2, waiting for transfers between devices, body(): lax.all_to_all(result_tile.astype(jnp.bfloat16), 'blk', split_axis=0, con...  24.4 us
  transfers between devices with their start and end apart: 12, of which 11 were waited for; matrix products, arithmetic and copies ran while one was open for 11% of the time, Pallas kernels for 0%

profile of v1, /device:TPU:0, one launch (start us, length us, event | category | flops | bytes accessed | tf_op | source)
XLA Modules:
  0.0 761.9 jit_solution(6585637910368741289)
XLA Ops:
  7.2 0.0 all-gather.11.cloned.1.call-start
  7.2 0.7 all-gather.11.cloned.1.call-update
  7.9 0.0 all-gather.17.cloned.1.call-start
  8.0 0.7 all-gather.17.cloned.1.call-update
  8.7 0.0 reduce-scatter.3.cloned.1.call-start
  8.7 84.3 %all-gather.11.cloned.1.call-done = bf16[512,4096]{1,0:T(8,128)(2,1)} async-done(((bf16[512,1024]{1,0:T(8,128)(2,1)}), bf16[512,4096]{1,0:T(8,128)(2,1)}) %all-gather.11.cloned.1.call-update) | async-done | bytes 4194320 | tf_op jit(solution)/shard_map/all_gather | solution.py:42
  93.0 9.1 %convolution_convert_fusion.1 = bf16[4096,1024]{1,0:T(8,128)(2,1)} fusion(bf16[512,4096]{1,0:T(8,128)(2,1)} %all-gather.11.cloned.1.call-done, bf16[512,1024]{1,0:T(8,128)(2,1)S(1)} %copy-done.1), kind=kOutput, calls=%fused_computation.3 | convolution fusion | flops 4299161600 | bytes 13631488 | tf_op jit(solution)/shard_map/dot_general | solution.py:55
  102.2 0.0 reduce-scatter.3.cloned.1.call-update
  102.2 0.0 reduce-scatter.5.cloned.1.call-start
  102.2 71.6 %all-gather.17.cloned.1.call-done = bf16[512,4096]{1,0:T(8,128)(2,1)} async-done(((bf16[512,1024]{1,0:T(8,128)(2,1)}), bf16[512,4096]{1,0:T(8,128)(2,1)}) %all-gather.17.cloned.1.call-update) | async-done | bytes 4194320 | tf_op jit(solution)/shard_map/all_gather | solution.py:43
  173.9 9.0 %convolution_convert_fusion = bf16[4096,1024]{1,0:T(8,128)(2,1)} fusion(bf16[512,4096]{1,0:T(8,128)(2,1)} %all-gather.17.cloned.1.call-done, bf16[512,1024]{1,0:T(8,128)(2,1)S(1)} %copy-done.2), kind=kOutput, calls=%fused_computation.2 | convolution fusion | flops 4299161600 | bytes 13631488 | tf_op jit(solution)/shard_map/dot_general | solution.py:55
  182.9 0.0 all-gather.25.cloned.1.call-start
  183.0 4.2 multiply_reduce_fusion
  187.1 1.0 copy-done
  188.2 0.9 multiply_reduce_fusion.1
  189.1 24.5 %all-reduce = (bf16[4096]{0:T(1024)(128)(2,1)S(1)}, bf16[4096]{0:T(1024)(128)(2,1)S(1)}) all-reduce(bf16[4096]{0:T(1024)(128)(2,1)S(1)} %multiply_reduce_fusion.1, bf16[4096]{0:T(1024)(128)(2,1)S(1)} %multiply_reduce_fusion), channel_id=1, replica_groups=mesh['tok'=8,'blk'=4] {'tok'}, use_global_device_ids=true, to_apply=%region_2.0 | all-reduce | flops 8192 | bytes 32768 | tf_op jit(solution)/shard_map/psum | solution.py:46
  213.6 0.1 dynamic-slice_multiply_fusion
  213.7 0.1 dynamic-slice_multiply_fusion.1
  213.8 33.8 %reduce-scatter.3.cloned.1.call-done = bf16[512,1024]{1,0:T(8,128)(2,1)} async-done(((bf16[4096,1024]{1,0:T(8,128)(2,1)}), bf16[512,1024]{1,0:T(8,128)(2,1)}) %reduce-scatter.3.cloned.1.call-update) | async-done | bytes 1048592 | tf_op jit(solution)/shard_map/reduce_scatter | solution.py:54
  247.6 74.8 %reduce-scatter.5.cloned.1.call-done = bf16[512,1024]{1,0:T(8,128)(2,1)} async-done(((bf16[4096,1024]{1,0:T(8,128)(2,1)}), bf16[512,1024]{1,0:T(8,128)(2,1)}) %reduce-scatter.5.cloned.1.call-update) | async-done | bytes 1048592 | tf_op jit(solution)/shard_map/reduce_scatter | solution.py:54
  322.4 3.8 multiply_convert_fusion
  326.3 0.0 all-gather.19.cloned.1.call-start
  326.3 0.5 all-gather.19.cloned.1.call-update
  326.8 0.0 all-gather.23.cloned.1.call-start
  326.9 0.7 all-gather.23.cloned.1.call-update
  327.6 0.0 all-gather.13.cloned.1.call-start
  327.6 0.7 all-gather.13.cloned.1.call-update
  328.3 0.0 all-gather.21.cloned.1.call-start
  328.4 78.8 %all-gather.25.cloned.1.call-done = bf16[2048,1024]{1,0:T(8,128)(2,1)} async-done(((bf16[512,1024]{1,0:T(8,128)(2,1)}), bf16[2048,1024]{1,0:T(8,128)(2,1)}) %all-gather.25.cloned.1.call-update) | async-done | bytes 4194320 | tf_op jit(solution)/shard_map/all_gather | solution.py:27
  407.2 6.2 copy.8
  413.4 48.9 %all-gather.19.cloned.1.call-done = bf16[4096,1024]{1,0:T(8,128)(2,1)} async-done(((bf16[512,1024]{1,0:T(8,128)(2,1)}), bf16[4096,1024]{1,0:T(8,128)(2,1)}) %all-gather.19.cloned.1.call-update) | async-done | bytes 8388624 | tf_op jit(solution)/shard_map/all_gather | solution.py:20
  462.3 10.9 %fusion.9 = (bf16[512,1024]{1,0:T(8,128)(2,1)}, f32[512,1024]{1,0:T(8,128)}) fusion(bf16[512,4096]{0,1:T(8,128)(2,1)} %bitcast.30, bf16[4096,1024]{1,0:T(8,128)(2,1)} %all-gather.19.cloned.1.call-done), kind=kOutput, calls=%fused_computation.26 | convolution fusion | flops 4295491584 | bytes 15728640 | tf_op jit(solution)/shard_map/dot_general | solution.py:18
  473.1 0.2 all-gather.15.cloned.1.call-start
  473.4 71.2 %all-gather.23.cloned.1.call-done = bf16[2048,1024]{1,0:T(8,128)(2,1)} async-done(((bf16[512,1024]{1,0:T(8,128)(2,1)}), bf16[2048,1024]{1,0:T(8,128)(2,1)}) %all-gather.23.cloned.1.call-update) | async-done | bytes 4194320 | tf_op jit(solution)/shard_map/all_gather | solution.py:27
  544.6 6.2 copy.6
  550.8 48.4 %all-gather.13.cloned.1.call-done = bf16[4096,1024]{1,0:T(8,128)(2,1)} async-done(((bf16[512,1024]{1,0:T(8,128)(2,1)}), bf16[4096,1024]{1,0:T(8,128)(2,1)}) %all-gather.13.cloned.1.call-update) | async-done | bytes 8388624 | tf_op jit(solution)/shard_map/all_gather | solution.py:20
  599.3 10.9 %fusion.8 = (bf16[512,1024]{1,0:T(8,128)(2,1)}, f32[512,1024]{1,0:T(8,128)}) fusion(bf16[512,4096]{0,1:T(8,128)(2,1)} %bitcast.32, bf16[4096,1024]{1,0:T(8,128)(2,1)} %all-gather.13.cloned.1.call-done), kind=kOutput, calls=%fused_computation.25 | convolution fusion | flops 4295491584 | bytes 15728640 | tf_op jit(solution)/shard_map/dot_general | solution.py:18
  610.2 45.2 %all-gather.21.cloned.1.call-done = bf16[4096,1024]{1,0:T(8,128)(2,1)} async-done(((bf16[512,1024]{1,0:T(8,128)(2,1)}), bf16[4096,1024]{1,0:T(8,128)(2,1)}) %all-gather.21.cloned.1.call-update) | async-done | bytes 8388624 | tf_op jit(solution)/shard_map/all_gather | solution.py:20
  655.4 11.1 %fusion.7 = bf16[512,1024]{1,0:T(8,128)(2,1)} fusion(f32[512,1024]{1,0:T(8,128)} %get-tuple-element.9, bf16[512,1024]{1,0:T(8,128)(2,1)S(1)} %copy-done.4, bf16[512,4096]{0,1:T(8,128)(2,1)} %bitcast.31, bf16[4096,1024]{1,0:T(8,128)(2,1)} %all-gather.21.cloned.1.call-done, f32[1024]{0:T(1024)S(1)} %dynamic_slice.15, f32[512]{0:T(512)S(1)} %dynamic-slice_multiply_fusion, ...), kind=kOutput, calls=%fused_computation.14 | convolution fusion | flops 4301783040 | bytes 16789504 | tf_op jit(solution)/shard_map/dot_general | solution.py:18
  666.6 4.7 all-to-all-start.1
  671.3 40.1 %all-gather.15.cloned.1.call-done = bf16[4096,1024]{1,0:T(8,128)(2,1)} async-done(((bf16[512,1024]{1,0:T(8,128)(2,1)}), bf16[4096,1024]{1,0:T(8,128)(2,1)}) %all-gather.15.cloned.1.call-update) | async-done | bytes 8388624 | tf_op jit(solution)/shard_map/all_gather | solution.py:20
  711.5 11.2 %fusion.4 = bf16[512,1024]{1,0:T(8,128)(2,1)} fusion(f32[512,1024]{1,0:T(8,128)} %get-tuple-element.7, bf16[512,1024]{1,0:T(8,128)(2,1)S(1)} %copy-done.3, bf16[512,4096]{0,1:T(8,128)(2,1)} %bitcast.33, bf16[4096,1024]{1,0:T(8,128)(2,1)} %all-gather.15.cloned.1.call-done, f32[1024]{0:T(1024)S(1)} %dynamic_slice.13, ...), kind=kOutput, calls=%fused_computation.11 | convolution fusion | flops 4301783040 | bytes 16789504 | tf_op jit(solution)/shard_map/dot_general | solution.py:18
  722.6 4.6 all-to-all-start
  727.2 0.2 convert_bitcast_fusion
  727.5 1.5 copy.11
  728.9 24.4 %all-to-all-done = bf16[4,128,1024]{2,1,0:T(8,128)(2,1)S(1)} async-done(((bf16[4,128,1024]{2,1,0:T(8,128)(2,1)}), bf16[4,128,1024]{2,1,0:T(8,128)(2,1)S(1)}, u32[]{:S(2)}, u32[]{:S(2)}) %all-to-all-start) | async-done | bytes 1048608 | tf_op jit(solution)/shard_map/all_to_all | solution.py:77
  753.4 0.2 convert_bitcast_fusion.1
  753.6 1.5 copy.10
  (19 shorter events, 0.1 us)
Async XLA Ops:
  7.2 85.9 %copy-start.1 = (bf16[512,1024]{1,0:T(8,128)(2,1)S(1)}, bf16[512,1024]{1,0:T(8,128)(2,1)}, u32[]{:S(2)}) copy-start(bf16[512,1024]{1,0:T(8,128)(2,1)} %param.2) | copy-start | bytes 3145732
  7.2 85.9 %all-gather.11.cloned.1.call-start = ((), (), s32[]{:S(2)}) async-start(), calls=%async_computation.4 | async-start | bytes 5242880 | tf_op jit(solution)/shard_map/all_gather | solution.py:42
  7.9 166.0 %all-gather.17.cloned.1.call-start = ((), (), s32[]{:S(2)}) async-start(), calls=%async_computation.8 | async-start | bytes 5242880 | tf_op jit(solution)/shard_map/all_gather | solution.py:43
  8.7 238.9 %reduce-scatter.3.cloned.1.call-start = ((), (), s32[]{:S(2)}) async-start(), calls=%async_computation.5 | async-start | bytes 9437184 | tf_op jit(solution)/shard_map/reduce_scatter | solution.py:54
  102.2 71.7 %copy-start.2 = (bf16[512,1024]{1,0:T(8,128)(2,1)S(1)}, bf16[512,1024]{1,0:T(8,128)(2,1)}, u32[]{:S(2)}) copy-start(bf16[512,1024]{1,0:T(8,128)(2,1)} %param.3) | copy-start | bytes 3145732
  102.2 220.2 %reduce-scatter.5.cloned.1.call-start = ((), (), s32[]{:S(2)}) async-start(), calls=%async_computation.9 | async-start | bytes 9437184 | tf_op jit(solution)/shard_map/reduce_scatter | solution.py:54
  182.9 224.3 %all-gather.25.cloned.1.call-start = ((), (), s32[]{:S(2)}) async-start(), calls=%async_computation.13 | async-start | bytes 5242880 | tf_op jit(solution)/shard_map/all_gather | solution.py:27
  183.0 5.2 copy-start
  326.3 136.0 %all-gather.19.cloned.1.call-start = ((), (), s32[]{:S(2)}) async-start(), calls=%async_computation.10 | async-start | bytes 9437184 | tf_op jit(solution)/shard_map/all_gather | solution.py:20
  326.8 217.8 %all-gather.23.cloned.1.call-start = ((), (), s32[]{:S(2)}) async-start(), calls=%async_computation.12 | async-start | bytes 5242880 | tf_op jit(solution)/shard_map/all_gather | solution.py:27
  327.6 271.7 %all-gather.13.cloned.1.call-start = ((), (), s32[]{:S(2)}) async-start(), calls=%async_computation.6 | async-start | bytes 9437184 | tf_op jit(solution)/shard_map/all_gather | solution.py:20
  328.3 327.1 %all-gather.21.cloned.1.call-start = ((), (), s32[]{:S(2)}) async-start(), calls=%async_computation.11 | async-start | bytes 9437184 | tf_op jit(solution)/shard_map/all_gather | solution.py:20
  473.1 238.3 %all-gather.15.cloned.1.call-start = ((), (), s32[]{:S(2)}) async-start(), calls=%async_computation.7 | async-start | bytes 9437184 | tf_op jit(solution)/shard_map/all_gather | solution.py:20
  599.3 56.2 %copy-start.4 = (bf16[512,1024]{1,0:T(8,128)(2,1)S(1)}, bf16[512,1024]{1,0:T(8,128)(2,1)}, u32[]{:S(2)}) copy-start(bf16[512,1024]{1,0:T(8,128)(2,1)} %reduce-scatter.5.cloned.1.call-done) | copy-start | bytes 3145732
  666.6 44.9 %copy-start.3 = (bf16[512,1024]{1,0:T(8,128)(2,1)S(1)}, bf16[512,1024]{1,0:T(8,128)(2,1)}, u32[]{:S(2)}) copy-start(bf16[512,1024]{1,0:T(8,128)(2,1)} %reduce-scatter.3.cloned.1.call-done) | copy-start | bytes 3145732
  666.6 56.0 %all-to-all-start.1 = ((bf16[4,128,1024]{2,1,0:T(8,128)(2,1)}), bf16[4,128,1024]{2,1,0:T(8,128)(2,1)S(1)}, u32[]{:S(2)}, u32[]{:S(2)}) async-start(bf16[4,128,1024]{2,1,0:T(8,128)(2,1)} %bitcast.10), calls=%async_computation.3 | async-start | bytes 2097152 | tf_op jit(solution)/shard_map/all_to_all | solution.py:77
  722.6 30.7 %all-to-all-start = ((bf16[4,128,1024]{2,1,0:T(8,128)(2,1)}), bf16[4,128,1024]{2,1,0:T(8,128)(2,1)S(1)}, u32[]{:S(2)}, u32[]{:S(2)}) async-start(bf16[4,128,1024]{2,1,0:T(8,128)(2,1)} %bitcast.4), calls=%async_computation.1 | async-start | bytes 2097152 | tf_op jit(solution)/shard_map/all_to_all | solution.py:77
Sparse Core Ops, SparseCore 0:
  9.6 83.4 all-gather.10
  94.6 79.2 all-gather.16
  177.3 70.1 reduce-scatter.2
  250.9 71.4 reduce-scatter.4
  326.4 80.7 all-gather.24
  409.5 52.7 all-gather.18
  463.8 80.7 all-gather.22
  546.5 52.7 all-gather.12
  601.2 54.2 all-gather.20
  657.2 54.2 all-gather.14
